TPU v7x, 32 devices: a whole 2x2x4 slice. The times are simulated.
32 devices in a mesh: gene: 8 (over z, x), cell: 4 (over y, core).
Axes of the slice: x: 2, y: 2, z: 4, core: 2. Of those that a mesh axis runs over, the one named last changes fastest.
Arguments:
- pool_counts: bfloat16 [20480, 16384], P('gene', 'cell'), may hold values from 0 to 6.5
- cell_picks: int32 [7, 4096], P(None, 'cell'), may hold values from 0 to 16383, as said below
- loadings_init: float32 [64, 20480], P(None, 'gene'), may hold values from -0.0390625 to 0.0390625
Outputs:
- scaled_loadings: float32 [64, 20480], P(None, 'gene')
Inputs may be any that keep to these rules, and one draw needn't show every extreme that they name: `cell_picks`: column b of every row names a pool cell in [(b // 1024) * 4096, (b // 1024 + 1) * 4096); no cell is named twice in one row.
All inputs are finite; a program needn't handle non-finite values.
Results may differ from a plain program's by a relative error of at most 0.018.
Values may be sent and summed in bfloat16 or wider, within the bound.
A program may use at most 128 MiB of HBM per device.

v0:
```python
import math
import jax
import jax.numpy as jnp
from jax import lax
from jax.sharding import PartitionSpec as P

STEPS = 7
step_rate = 1.0


def transposed_product(left, right):
    return lax.dot_general(
        left, right, (((1,), (1,)), ((), ())), preferred_element_type=jnp.float32
    )


def shards(pool_counts, cell_picks, loadings_init):
    loadings = loadings_init
    local_pool = pool_counts.shape[1]
    group = lax.axis_index("cell")
    batch_total = cell_picks.shape[1] * lax.axis_size("cell")
    gene_total = loadings.shape[1] * lax.axis_size("gene")
    for step_index in range(STEPS):
        chosen = cell_picks[step_index] - group * local_pool
        gathered = jnp.take(pool_counts, chosen, axis=1)
        weights_low = loadings.astype(jnp.bfloat16)
        product = jnp.dot(weights_low, gathered, preferred_element_type=jnp.float32)
        local_sums = jnp.sum(gathered, axis=1, dtype=jnp.float32)
        batch_means = lax.psum(local_sums, "cell") / batch_total
        shift = jnp.dot(
            weights_low.astype(jnp.float32), batch_means, precision=lax.Precision.HIGHEST
        )
        partial_value = product - shift[:, None]
        scores = lax.psum(partial_value, "gene")
        scores_low = scores.astype(jnp.bfloat16)
        raw_update = transposed_product(scores_low, gathered)
        row_totals = jnp.sum(scores_low, axis=1, dtype=jnp.float32)
        local_update = (raw_update - row_totals[:, None] * batch_means[None, :]) / batch_total
        update = lax.psum(local_update.astype(jnp.bfloat16), "cell").astype(jnp.float32)
        stepped = loadings + step_rate * update
        gram_part = jnp.dot(stepped, stepped.T, precision=lax.Precision.HIGHEST)
        gram_matrix = lax.psum(gram_part, "gene")
        factor = jnp.linalg.cholesky(gram_matrix)
        loadings = lax.linalg.triangular_solve(factor, stepped, left_side=True, lower=True)
    return loadings * math.sqrt(gene_total)


def solution(mesh):
    placed = (P("gene", "cell"), P(None, "cell"), P(None, "gene"))
    return jax.shard_map(
        shards, mesh=mesh, in_specs=placed, out_specs=P(None, "gene"), check_vma=False
    )
```

profile of v0, /device:TPU:0, one launch (start us, length us, event | category | flops | bytes accessed | tf_op | source)
XLA Modules:
  0.0 1143.4 jit_solution(7488319310404820462)
XLA Ops:
  7.8 25.9 %copy.4 = bf16[2560,4096]{0,1:T(8,128)(2,1)} copy(bf16[2560,4096]{1,0:T(8,128)(2,1)} %param.8) | data formatting | bytes 41943040 | tf_op args[0]
  33.7 20.2 %gather_fusion.6 = bf16[1024,2560]{1,0:T(8,128)(2,1)} fusion(bf16[2560,4096]{0,1:T(8,128)(2,1)} %copy.4, s32[1024]{0:T(1024)S(1)} %fusion.188), kind=kCustom, calls=%fused_computation.6.clone | custom fusion | bytes 10489856 | tf_op jit(solution)/shard_map/jit(_take)/gather | solution.py:25
  53.8 20.1 %gather_fusion.5 = bf16[1024,2560]{1,0:T(8,128)(2,1)} fusion(bf16[2560,4096]{0,1:T(8,128)(2,1)} %copy.4, s32[1024]{0:T(1024)S(1)} %fusion.187), kind=kCustom, calls=%fused_computation.5.clone | custom fusion | bytes 10489856 | tf_op jit(solution)/shard_map/jit(_take)/gather | solution.py:25
  73.9 20.5 %gather_fusion.4 = bf16[1024,2560]{1,0:T(8,128)(2,1)} fusion(bf16[2560,4096]{0,1:T(8,128)(2,1)} %copy.4, s32[1024]{0:T(1024)S(1)} %fusion.186), kind=kCustom, calls=%fused_computation.4.clone | custom fusion | bytes 10489856 | tf_op jit(solution)/shard_map/jit(_take)/gather | solution.py:25
  94.5 20.1 %gather_fusion.3 = bf16[1024,2560]{1,0:T(8,128)(2,1)} fusion(bf16[2560,4096]{0,1:T(8,128)(2,1)} %copy.4, s32[1024]{0:T(1024)S(1)} %fusion.185), kind=kCustom, calls=%fused_computation.3.clone | custom fusion | bytes 10489856 | tf_op jit(solution)/shard_map/jit(_take)/gather | solution.py:25
  114.6 20.2 %gather_fusion.2 = bf16[1024,2560]{1,0:T(8,128)(2,1)} fusion(bf16[2560,4096]{0,1:T(8,128)(2,1)} %copy.4, s32[1024]{0:T(1024)S(1)} %fusion.184), kind=kCustom, calls=%fused_computation.2.clone | custom fusion | bytes 10489856 | tf_op jit(solution)/shard_map/jit(_take)/gather | solution.py:25
  134.8 20.1 %gather_fusion.1 = bf16[1024,2560]{1,0:T(8,128)(2,1)} fusion(bf16[2560,4096]{0,1:T(8,128)(2,1)} %copy.4, s32[1024]{0:T(1024)S(1)} %fusion.183), kind=kCustom, calls=%fused_computation.1.clone | custom fusion | bytes 10489856 | tf_op jit(solution)/shard_map/jit(_take)/gather | solution.py:25
  154.9 20.1 %gather_fusion = bf16[1024,2560]{1,0:T(8,128)(2,1)} fusion(bf16[2560,4096]{0,1:T(8,128)(2,1)} %copy.4, s32[1024]{0:T(1024)S(1)} %fusion.182), kind=kCustom, calls=%fused_computation.clone | custom fusion | bytes 10489856 | tf_op jit(solution)/shard_map/jit(_take)/gather | solution.py:25
  179.3 7.3 convert_reduce_fusion
  186.6 5.4 convert_reduce_fusion.2
  195.6 33.5 %all-reduce.31.cloned.1.call-done = (f32[2560]{0:T(1024)}, f32[2560]{0:T(1024)}, f32[2560]{0:T(1024)}, f32[2560]{0:T(1024)}, f32[2560]{0:T(1024)}, /*index=5*/f32[2560]{0:T(1024)}, f32[2560]{0:T(1024)}) async-done(((f32[2560]{0:T(1024)}, f32[2560]{0:T(1024)}, f32[2560]{0:T(1024)}, f32[2560]{0:T(1024)}, f32[2560]{0:T(1024)}, /*index=5*/f32[2560]{0:T(1024)}, f32[2560]{0:T(1024)}), (f32[2560]{0:T(1024)}, ...) | async-done | bytes 71696 | tf_op jit(solution)/shard_map/psum | solution.py:29
  234.5 40.8 %all-reduce.32 = bf16[64,1024]{1,0:T(8,128)(2,1)S(1)} all-reduce(f32[64,1024]{1,0:T(8,128)S(1)} %fusion.94), channel_id=1, replica_groups=mesh['gene'=8,'cell'=4] {'gene'}, use_global_device_ids=true, to_apply=%region_2.4 | all-reduce | flops 65536 | bytes 393216 | tf_op jit(solution)/shard_map/psum | solution.py:34
  279.9 30.0 %all-reduce.17.cloned.1.call-done = bf16[64,2560]{1,0:T(8,128)(2,1)} async-done(((bf16[64,2560]{1,0:T(8,128)(2,1)}), bf16[64,2560]{1,0:T(8,128)(2,1)}) %all-reduce.17.cloned.1.call-update) | async-done | bytes 327696 | tf_op jit(solution)/shard_map/psum | solution.py:39
  311.8 37.1 %psum.199 = f32[64,64]{0,1:T(8,128)S(1)} all-reduce(f32[64,64]{0,1:T(8,128)S(1)} %fusion.116), channel_id=1, replica_groups=mesh['gene'=8,'cell'=4] {'gene'}, use_global_device_ids=true, to_apply=%region_5.7 | all-reduce | flops 4096 | bytes 32768 | tf_op jit(solution)/shard_map/psum | solution.py:42
  348.9 5.8 cholesky.119
  356.1 4.9 custom-call.11
  367.4 36.0 %all-reduce.33 = bf16[64,1024]{1,0:T(8,128)(2,1)S(1)} all-reduce(f32[64,1024]{1,0:T(8,128)S(1)} %fusion.97), channel_id=1, replica_groups=mesh['gene'=8,'cell'=4] {'gene'}, use_global_device_ids=true, to_apply=%region_10.0 | all-reduce | flops 65536 | bytes 393216 | tf_op jit(solution)/shard_map/psum | solution.py:34
  408.1 30.5 %all-reduce.19.cloned.1.call-done = bf16[64,2560]{1,0:T(8,128)(2,1)} async-done(((bf16[64,2560]{1,0:T(8,128)(2,1)}), bf16[64,2560]{1,0:T(8,128)(2,1)}) %all-reduce.19.cloned.1.call-update) | async-done | bytes 327696 | tf_op jit(solution)/shard_map/psum | solution.py:39
  440.4 37.6 %psum.203 = f32[64,64]{0,1:T(8,128)S(1)} all-reduce(f32[64,64]{0,1:T(8,128)S(1)} %fusion.118), channel_id=1, replica_groups=mesh['gene'=8,'cell'=4] {'gene'}, use_global_device_ids=true, to_apply=%region_13.0 | all-reduce | flops 4096 | bytes 32768 | tf_op jit(solution)/shard_map/psum | solution.py:42
  478.1 5.8 cholesky.130
  485.3 4.9 custom-call.12
  496.6 36.0 %all-reduce.34 = bf16[64,1024]{1,0:T(8,128)(2,1)S(1)} all-reduce(f32[64,1024]{1,0:T(8,128)S(1)} %fusion.100), channel_id=1, replica_groups=mesh['gene'=8,'cell'=4] {'gene'}, use_global_device_ids=true, to_apply=%region_16.0 | all-reduce | flops 65536 | bytes 393216 | tf_op jit(solution)/shard_map/psum | solution.py:34
  537.2 30.6 %all-reduce.21.cloned.1.call-done = bf16[64,2560]{1,0:T(8,128)(2,1)} async-done(((bf16[64,2560]{1,0:T(8,128)(2,1)}), bf16[64,2560]{1,0:T(8,128)(2,1)}) %all-reduce.21.cloned.1.call-update) | async-done | bytes 327696 | tf_op jit(solution)/shard_map/psum | solution.py:39
  569.7 37.1 %psum.207 = f32[64,64]{0,1:T(8,128)S(1)} all-reduce(f32[64,64]{0,1:T(8,128)S(1)} %fusion.120), channel_id=1, replica_groups=mesh['gene'=8,'cell'=4] {'gene'}, use_global_device_ids=true, to_apply=%region_19.0 | all-reduce | flops 4096 | bytes 32768 | tf_op jit(solution)/shard_map/psum | solution.py:42
  606.9 5.8 cholesky.141
  614.0 4.9 custom-call.13
  625.3 36.0 %all-reduce.35 = bf16[64,1024]{1,0:T(8,128)(2,1)S(1)} all-reduce(f32[64,1024]{1,0:T(8,128)S(1)} %fusion.103), channel_id=1, replica_groups=mesh['gene'=8,'cell'=4] {'gene'}, use_global_device_ids=true, to_apply=%region_22.0 | all-reduce | flops 65536 | bytes 393216 | tf_op jit(solution)/shard_map/psum | solution.py:34
  661.5 4.4 fusion.79
  666.2 30.4 %all-reduce.23.cloned.1.call-done = bf16[64,2560]{1,0:T(8,128)(2,1)} async-done(((bf16[64,2560]{1,0:T(8,128)(2,1)}), bf16[64,2560]{1,0:T(8,128)(2,1)}) %all-reduce.23.cloned.1.call-update) | async-done | bytes 327696 | tf_op jit(solution)/shard_map/psum | solution.py:39
  698.4 37.1 %psum.211 = f32[64,64]{0,1:T(8,128)S(1)} all-reduce(f32[64,64]{0,1:T(8,128)S(1)} %fusion.122), channel_id=1, replica_groups=mesh['gene'=8,'cell'=4] {'gene'}, use_global_device_ids=true, to_apply=%region_25.0 | all-reduce | flops 4096 | bytes 32768 | tf_op jit(solution)/shard_map/psum | solution.py:42
  735.6 5.8 cholesky.152
  742.8 4.9 custom-call.14
  754.0 36.0 %all-reduce.36 = bf16[64,1024]{1,0:T(8,128)(2,1)S(1)} all-reduce(f32[64,1024]{1,0:T(8,128)S(1)} %fusion.106), channel_id=1, replica_groups=mesh['gene'=8,'cell'=4] {'gene'}, use_global_device_ids=true, to_apply=%region_28.0 | all-reduce | flops 65536 | bytes 393216 | tf_op jit(solution)/shard_map/psum | solution.py:34
  794.6 30.7 %all-reduce.25.cloned.1.call-done = bf16[64,2560]{1,0:T(8,128)(2,1)} async-done(((bf16[64,2560]{1,0:T(8,128)(2,1)}), bf16[64,2560]{1,0:T(8,128)(2,1)}) %all-reduce.25.cloned.1.call-update) | async-done | bytes 327696 | tf_op jit(solution)/shard_map/psum | solution.py:39
  827.1 37.1 %psum.215 = f32[64,64]{0,1:T(8,128)S(1)} all-reduce(f32[64,64]{0,1:T(8,128)S(1)} %fusion.124), channel_id=1, replica_groups=mesh['gene'=8,'cell'=4] {'gene'}, use_global_device_ids=true, to_apply=%region_31.0 | all-reduce | flops 4096 | bytes 32768 | tf_op jit(solution)/shard_map/psum | solution.py:42
  864.3 5.8 cholesky.163
  871.5 4.9 custom-call.15
  882.8 36.2 %all-reduce.37 = bf16[64,1024]{1,0:T(8,128)(2,1)S(1)} all-reduce(f32[64,1024]{1,0:T(8,128)S(1)} %fusion.109), channel_id=1, replica_groups=mesh['gene'=8,'cell'=4] {'gene'}, use_global_device_ids=true, to_apply=%region_34.0 | all-reduce | flops 65536 | bytes 393216 | tf_op jit(solution)/shard_map/psum | solution.py:34
  923.6 30.5 %all-reduce.27.cloned.1.call-done = bf16[64,2560]{1,0:T(8,128)(2,1)} async-done(((bf16[64,2560]{1,0:T(8,128)(2,1)}), bf16[64,2560]{1,0:T(8,128)(2,1)}) %all-reduce.27.cloned.1.call-update) | async-done | bytes 327696 | tf_op jit(solution)/shard_map/psum | solution.py:39
  956.0 37.1 %psum.219 = f32[64,64]{0,1:T(8,128)S(1)} all-reduce(f32[64,64]{0,1:T(8,128)S(1)} %fusion.126), channel_id=1, replica_groups=mesh['gene'=8,'cell'=4] {'gene'}, use_global_device_ids=true, to_apply=%region_37.0 | all-reduce | flops 4096 | bytes 32768 | tf_op jit(solution)/shard_map/psum | solution.py:42
  993.2 5.8 cholesky.174
  1000.3 4.9 custom-call.16
  1011.6 35.9 %all-reduce.38 = bf16[64,1024]{1,0:T(8,128)(2,1)S(1)} all-reduce(f32[64,1024]{1,0:T(8,128)S(1)} %fusion.112), channel_id=1, replica_groups=mesh['gene'=8,'cell'=4] {'gene'}, use_global_device_ids=true, to_apply=%region_40.0 | all-reduce | flops 65536 | bytes 393216 | tf_op jit(solution)/shard_map/psum | solution.py:34
  1047.7 4.4 fusion.88
  1052.1 30.7 %all-reduce.29.cloned.1.call-done = bf16[64,2560]{1,0:T(8,128)(2,1)} async-done(((bf16[64,2560]{1,0:T(8,128)(2,1)}), bf16[64,2560]{1,0:T(8,128)(2,1)}) %all-reduce.29.cloned.1.call-update) | async-done | bytes 327696 | tf_op jit(solution)/shard_map/psum | solution.py:39
  1084.5 37.1 %psum.223 = f32[64,64]{0,1:T(8,128)S(1)} all-reduce(f32[64,64]{0,1:T(8,128)S(1)} %fusion.127), channel_id=1, replica_groups=mesh['gene'=8,'cell'=4] {'gene'}, use_global_device_ids=true, to_apply=%region_43.47 | all-reduce | flops 4096 | bytes 32768 | tf_op jit(solution)/shard_map/psum | solution.py:42
  1121.7 5.8 cholesky.185
  1128.9 4.9 custom-call.17
  (151 shorter events, 101.1 us)
Async XLA Ops:
  6.5 222.6 %all-reduce.31.cloned.1.call-start = ((), (), s32[]{:S(2)}) async-start(), calls=%async_computation.7 | async-start | bytes 172032 | tf_op jit(solution)/shard_map/psum | solution.py:29
  175.0 11.6 %slice-start = ((s8[5242880]{0:T(1024)(128)(4,1)}), s8[1048576]{0:T(1024)(128)(4,1)S(1)}, s32[]{:S(2)}) async-start(s8[5242880]{0:T(1024)(128)(4,1)} %bitcast.200), calls=%async_computation.8 | async-start | bytes 2097152
  179.3 7.3 slice-start.1
  179.3 12.7 %slice-start.2 = ((s8[5242880]{0:T(1024)(128)(4,1)}), s8[4194304]{0:T(1024)(128)(4,1)S(1)}, s32[]{:S(2)}) async-start(s8[5242880]{0:T(1024)(128)(4,1)} %bitcast.202), calls=%async_computation.10 | async-start | bytes 8388608
  179.3 12.7 %slice-start.4 = ((s8[5242880]{0:T(1024)(128)(4,1)}), s8[4194304]{0:T(1024)(128)(4,1)S(1)}, s32[]{:S(2)}) async-start(s8[5242880]{0:T(1024)(128)(4,1)} %bitcast.204), calls=%async_computation.12 | async-start | bytes 8388608
  186.6 5.4 slice-start.3
  186.6 5.4 slice-start.5
  192.0 37.8 %copy-start = (f32[64,2560]{1,0:T(8,128)S(1)}, f32[64,2560]{1,0:T(8,128)}, u32[]{:S(2)}) copy-start(f32[64,2560]{1,0:T(8,128)} %param.10) | copy-start | bytes 1966084
  195.6 114.4 %all-reduce.17.cloned.1.call-start = ((), (), s32[]{:S(2)}) async-start(), calls=%async_computation | async-start | bytes 655360 | tf_op jit(solution)/shard_map/psum | solution.py:39
  234.5 45.4 %copy-start.6 = (f32[2560]{0:T(1024)S(1)}, f32[2560]{0:T(1024)}, u32[]{:S(2)}) copy-start(f32[2560]{0:T(1024)} %get-tuple-element.8) | copy-start | bytes 30724
  279.8 158.7 %all-reduce.19.cloned.1.call-start = ((), (), s32[]{:S(2)}) async-start(), calls=%async_computation.1 | async-start | bytes 655360 | tf_op jit(solution)/shard_map/psum | solution.py:39
  367.4 40.6 %copy-start.5 = (f32[2560]{0:T(1024)S(1)}, f32[2560]{0:T(1024)}, u32[]{:S(2)}) copy-start(f32[2560]{0:T(1024)} %get-tuple-element.10) | copy-start | bytes 30724
  408.0 159.9 %all-reduce.21.cloned.1.call-start = ((), (), s32[]{:S(2)}) async-start(), calls=%async_computation.2 | async-start | bytes 655360 | tf_op jit(solution)/shard_map/psum | solution.py:39
  496.6 40.6 %copy-start.4 = (f32[2560]{0:T(1024)S(1)}, f32[2560]{0:T(1024)}, u32[]{:S(2)}) copy-start(f32[2560]{0:T(1024)} %get-tuple-element.11) | copy-start | bytes 30724
  537.1 159.4 %all-reduce.23.cloned.1.call-start = ((), (), s32[]{:S(2)}) async-start(), calls=%async_computation.3 | async-start | bytes 655360 | tf_op jit(solution)/shard_map/psum | solution.py:39
  625.3 40.8 %copy-start.3 = (f32[2560]{0:T(1024)S(1)}, f32[2560]{0:T(1024)}, u32[]{:S(2)}) copy-start(f32[2560]{0:T(1024)} %get-tuple-element.12) | copy-start | bytes 30724
  665.9 159.4 %all-reduce.25.cloned.1.call-start = ((), (), s32[]{:S(2)}) async-start(), calls=%async_computation.4 | async-start | bytes 655360 | tf_op jit(solution)/shard_map/psum | solution.py:39
  754.0 40.6 %copy-start.2 = (f32[2560]{0:T(1024)S(1)}, f32[2560]{0:T(1024)}, u32[]{:S(2)}) copy-start(f32[2560]{0:T(1024)} %get-tuple-element.13) | copy-start | bytes 30724
  794.5 159.6 %all-reduce.27.cloned.1.call-start = ((), (), s32[]{:S(2)}) async-start(), calls=%async_computation.5 | async-start | bytes 655360 | tf_op jit(solution)/shard_map/psum | solution.py:39
  882.8 40.9 %copy-start.1 = (f32[2560]{0:T(1024)S(1)}, f32[2560]{0:T(1024)}, u32[]{:S(2)}) copy-start(f32[2560]{0:T(1024)} %get-tuple-element.14) | copy-start | bytes 30724
  923.5 159.2 %all-reduce.29.cloned.1.call-start = ((), (), s32[]{:S(2)}) async-start(), calls=%async_computation.6 | async-start | bytes 655360 | tf_op jit(solution)/shard_map/psum | solution.py:39
Sparse Core Ops, SparseCore 0:
  195.7 33.3 all-reduce.30
  280.0 29.9 all-reduce.16
  408.1 30.4 all-reduce.18
  537.3 30.5 all-reduce.20
  666.0 30.5 all-reduce.22
  794.7 30.5 all-reduce.24
  923.7 30.4 all-reduce.26
  1052.2 30.4 all-reduce.28
where the time goes:
time: 1150 us; the launch traced here: 1140 us
  blocking collectives  517 us (45%)
  waiting for transfers between devices  247 us (21%)
  local copies, waits for them, and re-layouts  168 us (15%)
  other arithmetic  108 us (9%)
  matrix products  88.8 us (8%)
  between operations  14.4 us (1%)
    psum x7, blocking collectives, shards(): gram_matrix = lax.psum(gram_part, 'gene')  260 us
    psum x7, blocking collectives, shards(): scores = lax.psum(partial_value, 'gene')  257 us
    psum x7, waiting for transfers between devices, shards(): lax.psum(local_update.astype(jnp.bfloat16), 'cell').astype(jnp.float32)  213 us
    gather x7, local copies, waits for them, and re-layouts, shards(): gathered = jnp.take(pool_counts, chosen, axis=1)  141 us
    another operation x21, other arithmetic, shards(): factor = jnp.linalg.cholesky(gram_matrix)  45.6 us
    another operation x14, other arithmetic, shards(): lax.linalg.triangular_solve(factor, stepped, left_side=True, lower=True)  38.8 us
    psum x1, waiting for transfers between devices, shards(): batch_means = lax.psum(local_sums, 'cell') / batch_total  33.5 us
    dot_general x7, matrix products, transposed_product(): lax.dot_general(left, right, (((1,), (1,)), ((), ())), preferred_element_...  30.7 us
  transfers between devices with their start and end apart: 8, of which 8 were waited for; matrix products, arithmetic and copies ran while one was open for 0% of the time, Pallas kernels for 0%

commit v1 on v0

--- a/solution.py
+++ b/solution.py
@@ -6,6 +6,11 @@
 
 STEPS = 7
 step_rate = 1.0
+
+
+def gather_and_add(x, name):
+    parts = lax.all_gather(x, name)
+    return jnp.sum(parts, axis=0)
 
 
 def transposed_product(left, right):
@@ -36,7 +41,7 @@
         raw_update = transposed_product(scores_low, gathered)
         row_totals = jnp.sum(scores_low, axis=1, dtype=jnp.float32)
         local_update = (raw_update - row_totals[:, None] * batch_means[None, :]) / batch_total
-        update = lax.psum(local_update.astype(jnp.bfloat16), "cell").astype(jnp.float32)
+        update = gather_and_add(local_update.astype(jnp.bfloat16), "cell").astype(jnp.float32)
         stepped = loadings + step_rate * update
         gram_part = jnp.dot(stepped, stepped.T, precision=lax.Precision.HIGHEST)
         gram_matrix = lax.psum(gram_part, "gene")

time: 1150 us -> 1050 us (0.913)
  waiting for transfers between devices: 247 us -> 149 us
  matrix products: 88.8 us -> 74 us
    psum x7 -> x0, waiting for transfers between devices: 213 us -> none  [shards(): lax.psum(local_update.astype(jnp.bfloat16), 'cell').astype(jnp.float32)]
    all_gather x0 -> x7, waiting for transfers between devices: none -> 116 us  [gather_and_add(): parts = lax.all_gather(x, name)]
where the time goes in v1:
time: 1050 us; the launch traced here: 1040 us
  blocking collectives  518 us (49%)
  local copies, waits for them, and re-layouts  168 us (16%)
  waiting for transfers between devices  149 us (14%)
  other arithmetic  118 us (11%)
  matrix products  74 us (7%)
  between operations  14.4 us (1%)
    psum x7, blocking collectives, shards(): gram_matrix = lax.psum(gram_part, 'gene')  260 us
    psum x7, blocking collectives, shards(): scores = lax.psum(partial_value, 'gene')  257 us
    gather x7, local copies, waits for them, and re-layouts, shards(): gathered = jnp.take(pool_counts, chosen, axis=1)  141 us
    all_gather x7, waiting for transfers between devices, gather_and_add(): parts = lax.all_gather(x, name)  116 us
    another operation x21, other arithmetic, shards(): factor = jnp.linalg.cholesky(gram_matrix)  45.6 us
    another operation x14, other arithmetic, shards(): lax.linalg.triangular_solve(factor, stepped, left_side=True, lower=True)  38.8 us
    psum x1, waiting for transfers between devices, shards(): batch_means = lax.psum(local_sums, 'cell') / batch_total  33.5 us
    dot_general x7, matrix products, transposed_product(): lax.dot_general(left, right, (((1,), (1,)), ((), ())), preferred_element_...  30.8 us
  transfers between devices with their start and end apart: 8, of which 8 were waited for; matrix products, arithmetic and copies ran while one was open for 0% of the time, Pallas kernels for 0%

profile of v1, /device:TPU:0, one launch (start us, length us, event | category | flops | bytes accessed | tf_op | source)
XLA Modules:
  0.0 1042.1 jit_solution(1881611622029403148)
XLA Ops:
  7.8 25.9 %copy.4 = bf16[2560,4096]{0,1:T(8,128)(2,1)} copy(bf16[2560,4096]{1,0:T(8,128)(2,1)} %param.8) | data formatting | bytes 41943040 | tf_op args[0]
  33.7 20.2 %gather_fusion.6 = bf16[1024,2560]{1,0:T(8,128)(2,1)} fusion(bf16[2560,4096]{0,1:T(8,128)(2,1)} %copy.4, s32[1024]{0:T(1024)S(1)} %fusion.188), kind=kCustom, calls=%fused_computation.6.clone | custom fusion | bytes 10489856 | tf_op jit(solution)/shard_map/jit(_take)/gather | solution.py:30
  53.8 20.1 %gather_fusion.5 = bf16[1024,2560]{1,0:T(8,128)(2,1)} fusion(bf16[2560,4096]{0,1:T(8,128)(2,1)} %copy.4, s32[1024]{0:T(1024)S(1)} %fusion.187), kind=kCustom, calls=%fused_computation.5.clone | custom fusion | bytes 10489856 | tf_op jit(solution)/shard_map/jit(_take)/gather | solution.py:30
  73.9 20.5 %gather_fusion.4 = bf16[1024,2560]{1,0:T(8,128)(2,1)} fusion(bf16[2560,4096]{0,1:T(8,128)(2,1)} %copy.4, s32[1024]{0:T(1024)S(1)} %fusion.186), kind=kCustom, calls=%fused_computation.4.clone | custom fusion | bytes 10489856 | tf_op jit(solution)/shard_map/jit(_take)/gather | solution.py:30
  94.5 20.1 %gather_fusion.3 = bf16[1024,2560]{1,0:T(8,128)(2,1)} fusion(bf16[2560,4096]{0,1:T(8,128)(2,1)} %copy.4, s32[1024]{0:T(1024)S(1)} %fusion.185), kind=kCustom, calls=%fused_computation.3.clone | custom fusion | bytes 10489856 | tf_op jit(solution)/shard_map/jit(_take)/gather | solution.py:30
  114.6 20.2 %gather_fusion.2 = bf16[1024,2560]{1,0:T(8,128)(2,1)} fusion(bf16[2560,4096]{0,1:T(8,128)(2,1)} %copy.4, s32[1024]{0:T(1024)S(1)} %fusion.184), kind=kCustom, calls=%fused_computation.2.clone | custom fusion | bytes 10489856 | tf_op jit(solution)/shard_map/jit(_take)/gather | solution.py:30
  134.8 20.1 %gather_fusion.1 = bf16[1024,2560]{1,0:T(8,128)(2,1)} fusion(bf16[2560,4096]{0,1:T(8,128)(2,1)} %copy.4, s32[1024]{0:T(1024)S(1)} %fusion.183), kind=kCustom, calls=%fused_computation.1.clone | custom fusion | bytes 10489856 | tf_op jit(solution)/shard_map/jit(_take)/gather | solution.py:30
  154.9 20.1 %gather_fusion = bf16[1024,2560]{1,0:T(8,128)(2,1)} fusion(bf16[2560,4096]{0,1:T(8,128)(2,1)} %copy.4, s32[1024]{0:T(1024)S(1)} %fusion.182), kind=kCustom, calls=%fused_computation.clone | custom fusion | bytes 10489856 | tf_op jit(solution)/shard_map/jit(_take)/gather | solution.py:30
  179.3 7.3 convert_reduce_fusion
  186.6 5.4 convert_reduce_fusion.2
  195.6 33.5 %all-reduce.10.cloned.1.call-done = (f32[2560]{0:T(1024)}, f32[2560]{0:T(1024)}, f32[2560]{0:T(1024)}, f32[2560]{0:T(1024)}, f32[2560]{0:T(1024)}, /*index=5*/f32[2560]{0:T(1024)}, f32[2560]{0:T(1024)}) async-done(((f32[2560]{0:T(1024)}, f32[2560]{0:T(1024)}, f32[2560]{0:T(1024)}, f32[2560]{0:T(1024)}, f32[2560]{0:T(1024)}, /*index=5*/f32[2560]{0:T(1024)}, f32[2560]{0:T(1024)}), (f32[2560]{0:T(1024)}, ...) | async-done | bytes 71696 | tf_op jit(solution)/shard_map/psum | solution.py:34
  234.5 40.8 %all-reduce.11 = bf16[64,1024]{1,0:T(8,128)(2,1)S(1)} all-reduce(f32[64,1024]{1,0:T(8,128)S(1)} %fusion.94), channel_id=1, replica_groups=mesh['gene'=8,'cell'=4] {'gene'}, use_global_device_ids=true, to_apply=%region_2.4 | all-reduce | flops 65536 | bytes 393216 | tf_op jit(solution)/shard_map/psum | solution.py:39
  279.9 15.6 %all-gather.15.cloned.1.call-done = bf16[256,2560]{1,0:T(8,128)(2,1)} async-done(((bf16[64,2560]{1,0:T(8,128)(2,1)}), bf16[256,2560]{1,0:T(8,128)(2,1)}) %all-gather.15.cloned.1.call-update) | async-done | bytes 1310736 | tf_op jit(solution)/shard_map/all_gather | solution.py:12
  297.8 37.1 %psum.149 = f32[64,64]{0,1:T(8,128)S(1)} all-reduce(f32[64,64]{0,1:T(8,128)S(1)} %fusion.116), channel_id=1, replica_groups=mesh['gene'=8,'cell'=4] {'gene'}, use_global_device_ids=true, to_apply=%region_5.7 | all-reduce | flops 4096 | bytes 32768 | tf_op jit(solution)/shard_map/psum | solution.py:47
  335.0 5.8 cholesky.119
  342.2 4.9 custom-call.11
  352.5 35.9 %all-reduce.12 = bf16[64,1024]{1,0:T(8,128)(2,1)S(1)} all-reduce(f32[64,1024]{1,0:T(8,128)S(1)} %fusion.97), channel_id=1, replica_groups=mesh['gene'=8,'cell'=4] {'gene'}, use_global_device_ids=true, to_apply=%region_10.0 | all-reduce | flops 65536 | bytes 393216 | tf_op jit(solution)/shard_map/psum | solution.py:39
  393.0 16.8 %all-gather.17.cloned.1.call-done = bf16[256,2560]{1,0:T(8,128)(2,1)} async-done(((bf16[64,2560]{1,0:T(8,128)(2,1)}), bf16[256,2560]{1,0:T(8,128)(2,1)}) %all-gather.17.cloned.1.call-update) | async-done | bytes 1310736 | tf_op jit(solution)/shard_map/all_gather | solution.py:12
  412.0 37.6 %psum.152 = f32[64,64]{0,1:T(8,128)S(1)} all-reduce(f32[64,64]{0,1:T(8,128)S(1)} %fusion.118), channel_id=1, replica_groups=mesh['gene'=8,'cell'=4] {'gene'}, use_global_device_ids=true, to_apply=%region_13.0 | all-reduce | flops 4096 | bytes 32768 | tf_op jit(solution)/shard_map/psum | solution.py:47
  449.8 5.8 cholesky.130
  457.0 4.9 custom-call.12
  467.3 36.1 %all-reduce.13 = bf16[64,1024]{1,0:T(8,128)(2,1)S(1)} all-reduce(f32[64,1024]{1,0:T(8,128)S(1)} %fusion.100), channel_id=1, replica_groups=mesh['gene'=8,'cell'=4] {'gene'}, use_global_device_ids=true, to_apply=%region_16.0 | all-reduce | flops 65536 | bytes 393216 | tf_op jit(solution)/shard_map/psum | solution.py:39
  503.5 4.4 fusion.76
  508.0 16.4 %all-gather.19.cloned.1.call-done = bf16[256,2560]{1,0:T(8,128)(2,1)} async-done(((bf16[64,2560]{1,0:T(8,128)(2,1)}), bf16[256,2560]{1,0:T(8,128)(2,1)}) %all-gather.19.cloned.1.call-update) | async-done | bytes 1310736 | tf_op jit(solution)/shard_map/all_gather | solution.py:12
  526.6 37.1 %psum.155 = f32[64,64]{0,1:T(8,128)S(1)} all-reduce(f32[64,64]{0,1:T(8,128)S(1)} %fusion.120), channel_id=1, replica_groups=mesh['gene'=8,'cell'=4] {'gene'}, use_global_device_ids=true, to_apply=%region_19.0 | all-reduce | flops 4096 | bytes 32768 | tf_op jit(solution)/shard_map/psum | solution.py:47
  563.8 5.8 cholesky.141
  571.0 4.9 custom-call.13
  581.3 35.9 %all-reduce.14 = bf16[64,1024]{1,0:T(8,128)(2,1)S(1)} all-reduce(f32[64,1024]{1,0:T(8,128)S(1)} %fusion.103), channel_id=1, replica_groups=mesh['gene'=8,'cell'=4] {'gene'}, use_global_device_ids=true, to_apply=%region_22.0 | all-reduce | flops 65536 | bytes 393216 | tf_op jit(solution)/shard_map/psum | solution.py:39
  622.0 16.7 %all-gather.21.cloned.1.call-done = bf16[256,2560]{1,0:T(8,128)(2,1)} async-done(((bf16[64,2560]{1,0:T(8,128)(2,1)}), bf16[256,2560]{1,0:T(8,128)(2,1)}) %all-gather.21.cloned.1.call-update) | async-done | bytes 1310736 | tf_op jit(solution)/shard_map/all_gather | solution.py:12
  640.9 37.1 %psum.158 = f32[64,64]{0,1:T(8,128)S(1)} all-reduce(f32[64,64]{0,1:T(8,128)S(1)} %fusion.122), channel_id=1, replica_groups=mesh['gene'=8,'cell'=4] {'gene'}, use_global_device_ids=true, to_apply=%region_25.0 | all-reduce | flops 4096 | bytes 32768 | tf_op jit(solution)/shard_map/psum | solution.py:47
  678.1 5.8 cholesky.152
  685.3 4.9 custom-call.14
  695.6 36.1 %all-reduce.15 = bf16[64,1024]{1,0:T(8,128)(2,1)S(1)} all-reduce(f32[64,1024]{1,0:T(8,128)S(1)} %fusion.106), channel_id=1, replica_groups=mesh['gene'=8,'cell'=4] {'gene'}, use_global_device_ids=true, to_apply=%region_28.0 | all-reduce | flops 65536 | bytes 393216 | tf_op jit(solution)/shard_map/psum | solution.py:39
  731.8 4.4 fusion.82
  736.3 16.9 %all-gather.23.cloned.1.call-done = bf16[256,2560]{1,0:T(8,128)(2,1)} async-done(((bf16[64,2560]{1,0:T(8,128)(2,1)}), bf16[256,2560]{1,0:T(8,128)(2,1)}) %all-gather.23.cloned.1.call-update) | async-done | bytes 1310736 | tf_op jit(solution)/shard_map/all_gather | solution.py:12
  755.5 37.1 %psum.161 = f32[64,64]{0,1:T(8,128)S(1)} all-reduce(f32[64,64]{0,1:T(8,128)S(1)} %fusion.124), channel_id=1, replica_groups=mesh['gene'=8,'cell'=4] {'gene'}, use_global_device_ids=true, to_apply=%region_31.0 | all-reduce | flops 4096 | bytes 32768 | tf_op jit(solution)/shard_map/psum | solution.py:47
  792.7 5.8 cholesky.163
  799.9 4.9 custom-call.15
  810.2 36.3 %all-reduce.16 = bf16[64,1024]{1,0:T(8,128)(2,1)S(1)} all-reduce(f32[64,1024]{1,0:T(8,128)S(1)} %fusion.109), channel_id=1, replica_groups=mesh['gene'=8,'cell'=4] {'gene'}, use_global_device_ids=true, to_apply=%region_34.0 | all-reduce | flops 65536 | bytes 393216 | tf_op jit(solution)/shard_map/psum | solution.py:39
  851.1 16.9 %all-gather.25.cloned.1.call-done = bf16[256,2560]{1,0:T(8,128)(2,1)} async-done(((bf16[64,2560]{1,0:T(8,128)(2,1)}), bf16[256,2560]{1,0:T(8,128)(2,1)}) %all-gather.25.cloned.1.call-update) | async-done | bytes 1310736 | tf_op jit(solution)/shard_map/all_gather | solution.py:12
  870.3 37.1 %psum.164 = f32[64,64]{0,1:T(8,128)S(1)} all-reduce(f32[64,64]{0,1:T(8,128)S(1)} %fusion.126), channel_id=1, replica_groups=mesh['gene'=8,'cell'=4] {'gene'}, use_global_device_ids=true, to_apply=%region_37.0 | all-reduce | flops 4096 | bytes 32768 | tf_op jit(solution)/shard_map/psum | solution.py:47
  907.5 5.8 cholesky.174
  914.7 4.9 custom-call.16
  925.0 36.0 %all-reduce.17 = bf16[64,1024]{1,0:T(8,128)(2,1)S(1)} all-reduce(f32[64,1024]{1,0:T(8,128)S(1)} %fusion.112), channel_id=1, replica_groups=mesh['gene'=8,'cell'=4] {'gene'}, use_global_device_ids=true, to_apply=%region_40.0 | all-reduce | flops 65536 | bytes 393216 | tf_op jit(solution)/shard_map/psum | solution.py:39
  965.5 16.5 %all-gather.27.cloned.1.call-done = bf16[256,2560]{1,0:T(8,128)(2,1)} async-done(((bf16[64,2560]{1,0:T(8,128)(2,1)}), bf16[256,2560]{1,0:T(8,128)(2,1)}) %all-gather.27.cloned.1.call-update) | async-done | bytes 1310736 | tf_op jit(solution)/shard_map/all_gather | solution.py:12
  984.2 37.1 %psum.167 = f32[64,64]{0,1:T(8,128)S(1)} all-reduce(f32[64,64]{0,1:T(8,128)S(1)} %fusion.127), channel_id=1, replica_groups=mesh['gene'=8,'cell'=4] {'gene'}, use_global_device_ids=true, to_apply=%region_43.47 | all-reduce | flops 4096 | bytes 32768 | tf_op jit(solution)/shard_map/psum | solution.py:47
  1021.4 5.8 cholesky.185
  1028.6 4.9 custom-call.17
  (158 shorter events, 97.0 us)
Async XLA Ops:
  6.5 222.6 %all-reduce.10.cloned.1.call-start = ((), (), s32[]{:S(2)}) async-start(), calls=%async_computation.7 | async-start | bytes 172032 | tf_op jit(solution)/shard_map/psum | solution.py:34
  175.0 11.6 %slice-start = ((s8[5242880]{0:T(1024)(128)(4,1)}), s8[1048576]{0:T(1024)(128)(4,1)S(1)}, s32[]{:S(2)}) async-start(s8[5242880]{0:T(1024)(128)(4,1)} %bitcast.207), calls=%async_computation.8 | async-start | bytes 2097152
  179.3 7.3 slice-start.1
  179.3 12.7 %slice-start.2 = ((s8[5242880]{0:T(1024)(128)(4,1)}), s8[4194304]{0:T(1024)(128)(4,1)S(1)}, s32[]{:S(2)}) async-start(s8[5242880]{0:T(1024)(128)(4,1)} %bitcast.209), calls=%async_computation.10 | async-start | bytes 8388608
  179.3 12.7 %slice-start.4 = ((s8[5242880]{0:T(1024)(128)(4,1)}), s8[4194304]{0:T(1024)(128)(4,1)S(1)}, s32[]{:S(2)}) async-start(s8[5242880]{0:T(1024)(128)(4,1)} %bitcast.211), calls=%async_computation.12 | async-start | bytes 8388608
  186.6 5.4 slice-start.3
  186.6 5.4 slice-start.5
  192.0 37.8 %copy-start = (f32[64,2560]{1,0:T(8,128)S(1)}, f32[64,2560]{1,0:T(8,128)}, u32[]{:S(2)}) copy-start(f32[64,2560]{1,0:T(8,128)} %param.10) | copy-start | bytes 1966084
  195.6 100.0 %all-gather.15.cloned.1.call-start = ((), (), s32[]{:S(2)}) async-start(), calls=%async_computation | async-start | bytes 1638400 | tf_op jit(solution)/shard_map/all_gather | solution.py:12
  234.5 45.4 %copy-start.6 = (f32[2560]{0:T(1024)S(1)}, f32[2560]{0:T(1024)}, u32[]{:S(2)}) copy-start(f32[2560]{0:T(1024)} %get-tuple-element.8) | copy-start | bytes 30724
  279.8 130.0 %all-gather.17.cloned.1.call-start = ((), (), s32[]{:S(2)}) async-start(), calls=%async_computation.1 | async-start | bytes 1638400 | tf_op jit(solution)/shard_map/all_gather | solution.py:12
  352.5 40.5 %copy-start.5 = (f32[2560]{0:T(1024)S(1)}, f32[2560]{0:T(1024)}, u32[]{:S(2)}) copy-start(f32[2560]{0:T(1024)} %get-tuple-element.10) | copy-start | bytes 30724
  393.0 131.4 %all-gather.19.cloned.1.call-start = ((), (), s32[]{:S(2)}) async-start(), calls=%async_computation.2 | async-start | bytes 1638400 | tf_op jit(solution)/shard_map/all_gather | solution.py:12
  467.3 40.7 %copy-start.4 = (f32[2560]{0:T(1024)S(1)}, f32[2560]{0:T(1024)}, u32[]{:S(2)}) copy-start(f32[2560]{0:T(1024)} %get-tuple-element.11) | copy-start | bytes 30724
  508.0 130.7 %all-gather.21.cloned.1.call-start = ((), (), s32[]{:S(2)}) async-start(), calls=%async_computation.3 | async-start | bytes 1638400 | tf_op jit(solution)/shard_map/all_gather | solution.py:12
  581.3 40.6 %copy-start.3 = (f32[2560]{0:T(1024)S(1)}, f32[2560]{0:T(1024)}, u32[]{:S(2)}) copy-start(f32[2560]{0:T(1024)} %get-tuple-element.12) | copy-start | bytes 30724
  621.7 131.5 %all-gather.23.cloned.1.call-start = ((), (), s32[]{:S(2)}) async-start(), calls=%async_computation.4 | async-start | bytes 1638400 | tf_op jit(solution)/shard_map/all_gather | solution.py:12
  695.6 40.7 %copy-start.2 = (f32[2560]{0:T(1024)S(1)}, f32[2560]{0:T(1024)}, u32[]{:S(2)}) copy-start(f32[2560]{0:T(1024)} %get-tuple-element.13) | copy-start | bytes 30724
  736.2 131.8 %all-gather.25.cloned.1.call-start = ((), (), s32[]{:S(2)}) async-start(), calls=%async_computation.5 | async-start | bytes 1638400 | tf_op jit(solution)/shard_map/all_gather | solution.py:12
  810.2 40.9 %copy-start.1 = (f32[2560]{0:T(1024)S(1)}, f32[2560]{0:T(1024)}, u32[]{:S(2)}) copy-start(f32[2560]{0:T(1024)} %get-tuple-element.14) | copy-start | bytes 30724
  851.0 130.9 %all-gather.27.cloned.1.call-start = ((), (), s32[]{:S(2)}) async-start(), calls=%async_computation.6 | async-start | bytes 1638400 | tf_op jit(solution)/shard_map/all_gather | solution.py:12
Sparse Core Ops, SparseCore 0:
  195.7 33.3 all-reduce.9
  280.0 15.5 all-gather.14
  393.1 16.6 all-gather.16
  508.1 16.2 all-gather.18
  621.9 16.7 all-gather.20
  736.4 16.8 all-gather.22
  851.1 16.8 all-gather.24
  965.6 16.2 all-gather.26
